TPU v7x, 256 devices: a whole 4x4x8 slice. The times are simulated.
256 devices in a mesh: grp: 4 (over y), seq: 64 (over x, z, core).
Axes of the slice: x: 4, y: 4, z: 8, core: 2. Of those that a mesh axis runs over, the one named last changes fastest.
Arguments:
- queries: bfloat16 [65536, 2048], P(('grp', 'seq')), may hold values from -48 to 48
- key_rows: bfloat16 [65536, 512], P(('grp', 'seq')), may hold values from -4.5 to 4.5
- value_rows: bfloat16 [65536, 512], P(('grp', 'seq')), may hold values from -6 to 6
- segments: int32 [65536], P(('grp', 'seq')), may hold values from 0 to 30, as said below
Outputs:
- attended: bfloat16 [65536, 2048], P(('grp', 'seq'))
- log_sums: float32 [16, 65536], P(None, ('grp', 'seq'))
Inputs may be any that keep to these rules, and one draw needn't show every extreme that they name: `segments`: never falls along the sequence, starts at 0 and rises by one at each new document; the last token holds the largest value.
All inputs are finite; a program needn't handle non-finite values.
Results may differ from a plain program's by a relative error of at most 0.0035.
Values may be sent and summed in bfloat16 or wider, within the bound.
No kernel may reach another device: no remote copies, remote signals or barrier semaphores. Data moves between devices by JAX's collectives and lax.ppermute only.
A program may use at most 192 MiB of HBM per device.

v0:
```python
import math

import jax
import jax.numpy as jnp
from jax import lax
from jax.sharding import Mesh
from jax.sharding import PartitionSpec as P

Q_HEADS = 16
KV_HEADS = 4
HEAD_DIM = 128
WINDOW = 4096
GRP_SEQ = ("grp", "seq_0", "seq_1", "seq_2")


def filled_with(array, identity):
    return jax.tree.map(
        lambda a, e: jnp.broadcast_to(jnp.asarray(e, a.dtype), a.shape), array, identity
    )


def collected_together(array, axis):
    leaves = jax.tree.leaves(array)
    order = sorted(range(len(leaves)), key=lambda k: -leaves[k].size)
    width = (1, *leaves[order[0]].shape)[-1]
    lines = [
        jnp.pad(leaves[k].reshape(-1), (0, -leaves[k].size % width)).reshape(-1, width)
        for k in order
    ]
    both, at, found = (lax.all_gather(jnp.concatenate(lines), axis), 0, {})
    for k, line in zip(order, lines):
        slab = both[:, at : at + len(line)].reshape(len(both), -1)
        found[k] = slab[:, : leaves[k].size].reshape(-1, *leaves[k].shape)
        at += len(line)
    numbers = iter(range(len(leaves)))
    return jax.tree.map(lambda _: found[next(numbers)], array)


def prefix_by_axis(array, axes, combine, identity):
    before = start = filled_with(array, identity)
    total = array
    for axis in reversed(axes):
        peers, mine = (lax.axis_size(axis), lax.axis_index(axis))
        pieces = collected_together(total, axis)
        inside, total = (start, start)
        for k in range(peers):
            passed = k < mine
            total = combine(total, jax.tree.map(lambda part: part[k], pieces))
            inside = jax.tree.map(lambda new, old: jnp.where(passed, new, old), total, inside)
        before = combine(inside, before)
    return before


def from_behind(array, axis, by):
    peers = lax.axis_size(axis)
    pairs = [(i, i + by) for i in range(peers) if 0 <= i + by < peers]
    return lax.ppermute(array, axis, pairs)


def combine(earlier, later):
    a_begin, a_first, a_last, a_start = earlier
    b_begin, b_first, b_last, b_start = later
    start = jnp.where(b_start >= 0, b_start, jnp.where(b_first != a_last, b_begin, a_start))
    merged = (a_begin, a_first, b_last, start)
    return tuple(
        (
            jnp.where(a_begin < 0, bb, jnp.where(b_begin < 0, aa, mm))
            for aa, bb, mm in zip(earlier, later, merged)
        )
    )


def find_starts(segments, offset, tok):
    change = segments[1:] != segments[:-1]
    inner_pos = offset + jnp.arange(1, tok, dtype=jnp.int32)
    inner = jnp.max(jnp.where(change, inner_pos, -1))
    mine = (offset, segments[0], segments[tok - 1], inner)
    minus = jnp.int32(-1)
    prefix = prefix_by_axis(mine, GRP_SEQ, combine, (minus, minus, minus, minus))
    p_begin, p_first, p_last, p_start = prefix
    carried = jnp.where(p_begin < 0, 0, jnp.where(p_start >= 0, p_start, p_begin)).astype(jnp.int32)
    head_flag = (p_begin >= 0) & (segments[0] != p_last)
    flags = jnp.concatenate([head_flag[None], change])
    marks = jnp.where(flags, offset + jnp.arange(tok, dtype=jnp.int32), -1)
    return jnp.maximum(lax.cummax(marks, axis=0), carried)


def attend(state, q_heads, key_block, value_block, key_first, positions, lower):
    length = key_block.shape[0]
    k_heads = key_block.reshape(length, KV_HEADS, HEAD_DIM)
    v_heads = value_block.reshape(length, KV_HEADS, HEAD_DIM)
    scale = 1.0 / math.sqrt(HEAD_DIM)
    top, total, summed = state
    scores = (
        jnp.einsum("tkgd,lkd->kgtl", q_heads, k_heads, preferred_element_type=jnp.float32) * scale
    )
    key_pos = key_first + jnp.arange(length, dtype=jnp.int32)
    allowed = (key_pos[None, :] >= lower[:, None]) & (key_pos[None, :] <= positions[:, None])
    masked = jnp.where(allowed, scores, -1e30)
    top_new = jnp.maximum(top, jnp.max(masked, axis=-1))
    expo = jnp.where(allowed, jnp.exp(masked - top_new[..., None]), 0.0)
    factor = jnp.exp(top - top_new)
    total_new = total * factor + jnp.sum(expo, axis=-1)
    weights = expo.astype(jnp.bfloat16)
    update = jnp.einsum("kgtl,lkd->tkgd", weights, v_heads, preferred_element_type=jnp.float32)
    summed_new = summed * jnp.transpose(factor, (2, 0, 1))[..., None] + update
    return (top_new, total_new, summed_new)


def on_device(queries, key_rows, value_rows, segments):
    tok = queries.shape[0]
    group = Q_HEADS // KV_HEADS
    device = lax.axis_index(GRP_SEQ)
    offset = device * tok
    starts = find_starts(segments, offset, tok)
    positions = offset + jnp.arange(tok, dtype=jnp.int32)
    lower = jnp.maximum(starts, positions - WINDOW + 1)
    q_heads = queries.reshape(tok, KV_HEADS, group, HEAD_DIM)
    state = (
        jnp.full((KV_HEADS, group, tok), -1e30, jnp.float32),
        jnp.zeros((KV_HEADS, group, tok), jnp.float32),
        jnp.zeros((tok, KV_HEADS, group, HEAD_DIM), jnp.float32),
    )
    state = attend(state, q_heads, key_rows, value_rows, offset, positions, lower)
    reach = (WINDOW - 1) // tok + 1

    def one_step(turn, carry):
        blocks, current = carry
        blocks = from_behind((blocks[0], blocks[1]), GRP_SEQ, 1)
        key_first = offset - (turn + 1) * tok
        current = attend(current, q_heads, blocks[0], blocks[1], key_first, positions, lower)
        return (blocks, current)

    final = lax.fori_loop(0, reach, one_step, ((key_rows, value_rows), state))
    state = final[1]
    top, total, summed = state
    attended = (
        (summed / jnp.transpose(total, (2, 0, 1))[..., None])
        .reshape(tok, Q_HEADS * HEAD_DIM)
        .astype(jnp.bfloat16)
    )
    log_sums = (top + jnp.log(total)).reshape(Q_HEADS, tok)
    return (attended, log_sums)


def solution(mesh):
    split = Mesh(
        mesh.devices.reshape(mesh.shape["grp"], 4, 8, 2), ("grp", "seq_0", "seq_1", "seq_2")
    )
    placed = (P(GRP_SEQ, None), P(GRP_SEQ, None), P(GRP_SEQ, None), P(GRP_SEQ))
    return jax.shard_map(
        on_device,
        mesh=split,
        in_specs=placed,
        out_specs=(P(GRP_SEQ, None), P(None, GRP_SEQ)),
        check_vma=False,
    )
```

profile of v0, /device:TPU:8, one launch (start us, length us, event | category | flops | bytes accessed | tf_op | source)
XLA Modules:
  0.0 472.1 jit_solution(119159346198983746)
XLA Ops:
  5.4 2.0 fusion.36
  22.6 16.1 %all-reduce.1 = s32[32]{0:T(128)S(1)} all-reduce(s32[32]{0:T(128)S(1)} %fusion.37), channel_id=3, replica_groups=mesh['grp'=4,'seq_0'=4,'seq_1'=8,'seq_2'=2] {'seq_1'}, use_global_device_ids=true, to_apply=%add.1 | all-reduce | flops 32 | bytes 256
  90.9 8.9 %all-reduce.2 = s32[16]{0:T(128)S(1)} all-reduce(s32[16]{0:T(128)S(1)} %fusion.38), channel_id=4, replica_groups=mesh['grp'=4,'seq_0'=4,'seq_1'=8,'seq_2'=2] {'seq_0'}, use_global_device_ids=true, to_apply=%add.2 | all-reduce | flops 16 | bytes 128
  130.2 8.2 %all-reduce.3 = s32[16]{0:T(128)S(1)} all-reduce(s32[16]{0:T(128)S(1)} %fusion.39), channel_id=5, replica_groups=mesh['grp'=4,'seq_0'=4,'seq_1'=8,'seq_2'=2] {'grp'}, use_global_device_ids=true, to_apply=%add.3 | all-reduce | flops 16 | bytes 128
  173.3 5.3 %bitcast_add_fusion.1 = f32[256,4,4,128]{3,0,2,1:T(8,128)} fusion(f32[4,256,256,4]{2,1,3,0:T(8,128)} %copy-done, f32[4,4,256]{2,1,0:T(4,128)S(1)} %broadcast_maximum_fusion, pred[256,256]{0,1:T(8,128)(4,1)S(1)} %compare_and_fusion.1, f32[256,4,4]{0,2,1:T(4,128)S(1)} %get-tuple-element.256, bf16[256,4,128,1]{2,1,0,3:T(4,128)(2,1)S(1)} %bitcast.218), kind=kOutput, calls=%fused_computation.28 | convolution fusion | flops 274202624 | bytes 6651904 | tf_op jit(solution)/shard_map/kgtl,lkd->tkgd/dot_general | solution.py:105
  179.6 287.6 %while.23 = (s32[]{:T(128)}, bf16[256,512]{0,1:T(8,128)(2,1)S(1)}, bf16[256,512]{0,1:T(8,128)(2,1)S(1)}, f32[4,4,256]{2,1,0:T(4,128)S(1)}, f32[4,4,256]{2,1,0:T(...) while((s32[]{:T(128)}, bf16[256,512]{0,1:T(8,128)(2,1)S(1)}, ...), condition=%wide.region_8.9_spmd.clone.clone, body=%wide.region_5.8_spmd.clone.clone.sunk | while | flops 551760384 | bytes 38802708 | solution.py:134
  179.6 1.9 collective-permute-start
  181.5 3.0 collective-permute-start.1
  184.7 6.8 %collective-permute-done = bf16[256,512]{0,1:T(8,128)(2,1)S(1)} collective-permute-done((bf16[256,512]{0,1:T(8,128)(2,1)S(1)}, bf16[256,512]{0,1:T(8,128)(2,1)S(1)}, u32[]{:S(2)}, u32[]{:S(2)}) %collective-permute-start) | collective-permute-done | bytes 262176 | tf_op jit(solution)/shard_map/while/body/eval_jaxpr/ppermute | solution.py:57
  194.3 1.9 bitcast_add_fusion.3
  199.5 1.9 collective-permute-start.1
  201.6 7.9 %collective-permute-done = bf16[256,512]{0,1:T(8,128)(2,1)S(1)} collective-permute-done((bf16[256,512]{0,1:T(8,128)(2,1)S(1)}, bf16[256,512]{0,1:T(8,128)(2,1)S(1)}, u32[]{:S(2)}, u32[]{:S(2)}) %collective-permute-start) | collective-permute-done | bytes 262176 | tf_op jit(solution)/shard_map/while/body/eval_jaxpr/ppermute | solution.py:57
  212.3 1.9 bitcast_add_fusion.3
  217.5 1.9 collective-permute-start.1
  219.5 7.9 %collective-permute-done = bf16[256,512]{0,1:T(8,128)(2,1)S(1)} collective-permute-done((bf16[256,512]{0,1:T(8,128)(2,1)S(1)}, bf16[256,512]{0,1:T(8,128)(2,1)S(1)}, u32[]{:S(2)}, u32[]{:S(2)}) %collective-permute-start) | collective-permute-done | bytes 262176 | tf_op jit(solution)/shard_map/while/body/eval_jaxpr/ppermute | solution.py:57
  230.3 1.9 bitcast_add_fusion.3
  235.4 1.9 collective-permute-start.1
  237.5 7.9 %collective-permute-done = bf16[256,512]{0,1:T(8,128)(2,1)S(1)} collective-permute-done((bf16[256,512]{0,1:T(8,128)(2,1)S(1)}, bf16[256,512]{0,1:T(8,128)(2,1)S(1)}, u32[]{:S(2)}, u32[]{:S(2)}) %collective-permute-start) | collective-permute-done | bytes 262176 | tf_op jit(solution)/shard_map/while/body/eval_jaxpr/ppermute | solution.py:57
  248.2 1.9 bitcast_add_fusion.3
  255.5 7.9 %collective-permute-done = bf16[256,512]{0,1:T(8,128)(2,1)S(1)} collective-permute-done((bf16[256,512]{0,1:T(8,128)(2,1)S(1)}, bf16[256,512]{0,1:T(8,128)(2,1)S(1)}, u32[]{:S(2)}, u32[]{:S(2)}) %collective-permute-start) | collective-permute-done | bytes 262176 | tf_op jit(solution)/shard_map/while/body/eval_jaxpr/ppermute | solution.py:57
  266.2 1.9 bitcast_add_fusion.3
  273.5 7.9 %collective-permute-done = bf16[256,512]{0,1:T(8,128)(2,1)S(1)} collective-permute-done((bf16[256,512]{0,1:T(8,128)(2,1)S(1)}, bf16[256,512]{0,1:T(8,128)(2,1)S(1)}, u32[]{:S(2)}, u32[]{:S(2)}) %collective-permute-start) | collective-permute-done | bytes 262176 | tf_op jit(solution)/shard_map/while/body/eval_jaxpr/ppermute | solution.py:57
  284.2 1.9 bitcast_add_fusion.3
  289.3 1.9 collective-permute-start.1
  291.4 7.9 %collective-permute-done = bf16[256,512]{0,1:T(8,128)(2,1)S(1)} collective-permute-done((bf16[256,512]{0,1:T(8,128)(2,1)S(1)}, bf16[256,512]{0,1:T(8,128)(2,1)S(1)}, u32[]{:S(2)}, u32[]{:S(2)}) %collective-permute-start) | collective-permute-done | bytes 262176 | tf_op jit(solution)/shard_map/while/body/eval_jaxpr/ppermute | solution.py:57
  302.1 1.9 bitcast_add_fusion.3
  309.4 7.9 %collective-permute-done = bf16[256,512]{0,1:T(8,128)(2,1)S(1)} collective-permute-done((bf16[256,512]{0,1:T(8,128)(2,1)S(1)}, bf16[256,512]{0,1:T(8,128)(2,1)S(1)}, u32[]{:S(2)}, u32[]{:S(2)}) %collective-permute-start) | collective-permute-done | bytes 262176 | tf_op jit(solution)/shard_map/while/body/eval_jaxpr/ppermute | solution.py:57
  320.1 1.9 bitcast_add_fusion.3
  327.4 7.9 %collective-permute-done = bf16[256,512]{0,1:T(8,128)(2,1)S(1)} collective-permute-done((bf16[256,512]{0,1:T(8,128)(2,1)S(1)}, bf16[256,512]{0,1:T(8,128)(2,1)S(1)}, u32[]{:S(2)}, u32[]{:S(2)}) %collective-permute-start) | collective-permute-done | bytes 262176 | tf_op jit(solution)/shard_map/while/body/eval_jaxpr/ppermute | solution.py:57
  338.1 1.9 bitcast_add_fusion.3
  343.3 1.9 collective-permute-start.1
  345.3 7.9 %collective-permute-done = bf16[256,512]{0,1:T(8,128)(2,1)S(1)} collective-permute-done((bf16[256,512]{0,1:T(8,128)(2,1)S(1)}, bf16[256,512]{0,1:T(8,128)(2,1)S(1)}, u32[]{:S(2)}, u32[]{:S(2)}) %collective-permute-start) | collective-permute-done | bytes 262176 | tf_op jit(solution)/shard_map/while/body/eval_jaxpr/ppermute | solution.py:57
  356.1 1.9 bitcast_add_fusion.3
  363.3 7.9 %collective-permute-done = bf16[256,512]{0,1:T(8,128)(2,1)S(1)} collective-permute-done((bf16[256,512]{0,1:T(8,128)(2,1)S(1)}, bf16[256,512]{0,1:T(8,128)(2,1)S(1)}, u32[]{:S(2)}, u32[]{:S(2)}) %collective-permute-start) | collective-permute-done | bytes 262176 | tf_op jit(solution)/shard_map/while/body/eval_jaxpr/ppermute | solution.py:57
  374.0 1.9 bitcast_add_fusion.3
  381.3 7.9 %collective-permute-done = bf16[256,512]{0,1:T(8,128)(2,1)S(1)} collective-permute-done((bf16[256,512]{0,1:T(8,128)(2,1)S(1)}, bf16[256,512]{0,1:T(8,128)(2,1)S(1)}, u32[]{:S(2)}, u32[]{:S(2)}) %collective-permute-start) | collective-permute-done | bytes 262176 | tf_op jit(solution)/shard_map/while/body/eval_jaxpr/ppermute | solution.py:57
  392.0 1.9 bitcast_add_fusion.3
  397.2 1.9 collective-permute-start.1
  399.2 7.9 %collective-permute-done = bf16[256,512]{0,1:T(8,128)(2,1)S(1)} collective-permute-done((bf16[256,512]{0,1:T(8,128)(2,1)S(1)}, bf16[256,512]{0,1:T(8,128)(2,1)S(1)}, u32[]{:S(2)}, u32[]{:S(2)}) %collective-permute-start) | collective-permute-done | bytes 262176 | tf_op jit(solution)/shard_map/while/body/eval_jaxpr/ppermute | solution.py:57
  410.0 1.9 bitcast_add_fusion.3
  417.2 7.9 %collective-permute-done = bf16[256,512]{0,1:T(8,128)(2,1)S(1)} collective-permute-done((bf16[256,512]{0,1:T(8,128)(2,1)S(1)}, bf16[256,512]{0,1:T(8,128)(2,1)S(1)}, u32[]{:S(2)}, u32[]{:S(2)}) %collective-permute-start) | collective-permute-done | bytes 262176 | tf_op jit(solution)/shard_map/while/body/eval_jaxpr/ppermute | solution.py:57
  427.9 1.9 bitcast_add_fusion.3
  435.2 7.9 %collective-permute-done = bf16[256,512]{0,1:T(8,128)(2,1)S(1)} collective-permute-done((bf16[256,512]{0,1:T(8,128)(2,1)S(1)}, bf16[256,512]{0,1:T(8,128)(2,1)S(1)}, u32[]{:S(2)}, u32[]{:S(2)}) %collective-permute-start) | collective-permute-done | bytes 262176 | tf_op jit(solution)/shard_map/while/body/eval_jaxpr/ppermute | solution.py:57
  445.9 1.9 bitcast_add_fusion.3
  451.1 1.9 collective-permute-start.1
  453.2 7.9 %collective-permute-done = bf16[256,512]{0,1:T(8,128)(2,1)S(1)} collective-permute-done((bf16[256,512]{0,1:T(8,128)(2,1)S(1)}, bf16[256,512]{0,1:T(8,128)(2,1)S(1)}, u32[]{:S(2)}, u32[]{:S(2)}) %collective-permute-start) | collective-permute-done | bytes 262176 | tf_op jit(solution)/shard_map/while/body/eval_jaxpr/ppermute | solution.py:57
  463.9 1.9 bitcast_add_fusion.3
  467.8 1.9 divide_convert_fusion
  (298 shorter events, 136.7 us)
Async XLA Ops:
  169.4 3.8 copy-start.4
  173.3 6.0 %copy-start.3 = (bf16[256,512]{1,0:T(8,128)(2,1)S(1)}, bf16[256,512]{1,0:T(8,128)(2,1)}, u32[]{:S(2)}) copy-start(bf16[256,512]{1,0:T(8,128)(2,1)} %param.7) | copy-start | bytes 786436
  179.6 11.9 %collective-permute-start = (bf16[256,512]{0,1:T(8,128)(2,1)S(1)}, bf16[256,512]{0,1:T(8,128)(2,1)S(1)}, u32[]{:S(2)}, u32[]{:S(2)}) collective-permute-start(bf16[256,512]{0,1:T(8,128)(2,1)S(1)} %get-tuple-element.412), channel_id=1, source_target_pairs={{0,1},{1,2},{2,3},{3,4},{4,5},{5,6},{6,7},{7,8},{8,9},{9,10},{10,1... | collective-permute-start | bytes 786440 | tf_op jit(solution)/shard_map/while/body/eval_jaxpr/ppermute | solution.py:57
  181.5 12.8 %collective-permute-start.1 = (bf16[256,512]{0,1:T(8,128)(2,1)S(1)}, bf16[256,512]{0,1:T(8,128)(2,1)S(1)}, u32[]{:S(2)}, u32[]{:S(2)}) collective-permute-start(bf16[256,512]{0,1:T(8,128)(2,1)S(1)} %get-tuple-element.413), channel_id=1, source_target_pairs={{0,1},{1,2},{2,3},{3,4},{4,5},{5,6},{6,7},{7,8},{8,9},{9,10},{10,1... | collective-permute-start | bytes 786440 | tf_op jit(solution)/shard_map/while/body/eval_jaxpr/ppermute | solution.py:57
  191.5 2.8 copy-start.1
  197.6 11.9 %collective-permute-start = (bf16[256,512]{0,1:T(8,128)(2,1)S(1)}, bf16[256,512]{0,1:T(8,128)(2,1)S(1)}, u32[]{:S(2)}, u32[]{:S(2)}) collective-permute-start(bf16[256,512]{0,1:T(8,128)(2,1)S(1)} %get-tuple-element.412), channel_id=1, source_target_pairs={{0,1},{1,2},{2,3},{3,4},{4,5},{5,6},{6,7},{7,8},{8,9},{9,10},{10,1... | collective-permute-start | bytes 786440 | tf_op jit(solution)/shard_map/while/body/eval_jaxpr/ppermute | solution.py:57
  199.5 12.8 %collective-permute-start.1 = (bf16[256,512]{0,1:T(8,128)(2,1)S(1)}, bf16[256,512]{0,1:T(8,128)(2,1)S(1)}, u32[]{:S(2)}, u32[]{:S(2)}) collective-permute-start(bf16[256,512]{0,1:T(8,128)(2,1)S(1)} %get-tuple-element.413), channel_id=1, source_target_pairs={{0,1},{1,2},{2,3},{3,4},{4,5},{5,6},{6,7},{7,8},{8,9},{9,10},{10,1... | collective-permute-start | bytes 786440 | tf_op jit(solution)/shard_map/while/body/eval_jaxpr/ppermute | solution.py:57
  209.5 2.8 copy-start.1
  215.6 11.9 %collective-permute-start = (bf16[256,512]{0,1:T(8,128)(2,1)S(1)}, bf16[256,512]{0,1:T(8,128)(2,1)S(1)}, u32[]{:S(2)}, u32[]{:S(2)}) collective-permute-start(bf16[256,512]{0,1:T(8,128)(2,1)S(1)} %get-tuple-element.412), channel_id=1, source_target_pairs={{0,1},{1,2},{2,3},{3,4},{4,5},{5,6},{6,7},{7,8},{8,9},{9,10},{10,1... | collective-permute-start | bytes 786440 | tf_op jit(solution)/shard_map/while/body/eval_jaxpr/ppermute | solution.py:57
  217.5 12.8 %collective-permute-start.1 = (bf16[256,512]{0,1:T(8,128)(2,1)S(1)}, bf16[256,512]{0,1:T(8,128)(2,1)S(1)}, u32[]{:S(2)}, u32[]{:S(2)}) collective-permute-start(bf16[256,512]{0,1:T(8,128)(2,1)S(1)} %get-tuple-element.413), channel_id=1, source_target_pairs={{0,1},{1,2},{2,3},{3,4},{4,5},{5,6},{6,7},{7,8},{8,9},{9,10},{10,1... | collective-permute-start | bytes 786440 | tf_op jit(solution)/shard_map/while/body/eval_jaxpr/ppermute | solution.py:57
  227.4 2.8 copy-start.1
  233.5 11.9 %collective-permute-start = (bf16[256,512]{0,1:T(8,128)(2,1)S(1)}, bf16[256,512]{0,1:T(8,128)(2,1)S(1)}, u32[]{:S(2)}, u32[]{:S(2)}) collective-permute-start(bf16[256,512]{0,1:T(8,128)(2,1)S(1)} %get-tuple-element.412), channel_id=1, source_target_pairs={{0,1},{1,2},{2,3},{3,4},{4,5},{5,6},{6,7},{7,8},{8,9},{9,10},{10,1... | collective-permute-start | bytes 786440 | tf_op jit(solution)/shard_map/while/body/eval_jaxpr/ppermute | solution.py:57
  235.4 12.8 %collective-permute-start.1 = (bf16[256,512]{0,1:T(8,128)(2,1)S(1)}, bf16[256,512]{0,1:T(8,128)(2,1)S(1)}, u32[]{:S(2)}, u32[]{:S(2)}) collective-permute-start(bf16[256,512]{0,1:T(8,128)(2,1)S(1)} %get-tuple-element.413), channel_id=1, source_target_pairs={{0,1},{1,2},{2,3},{3,4},{4,5},{5,6},{6,7},{7,8},{8,9},{9,10},{10,1... | collective-permute-start | bytes 786440 | tf_op jit(solution)/shard_map/while/body/eval_jaxpr/ppermute | solution.py:57
  245.4 2.8 copy-start.1
  251.5 11.9 %collective-permute-start = (bf16[256,512]{0,1:T(8,128)(2,1)S(1)}, bf16[256,512]{0,1:T(8,128)(2,1)S(1)}, u32[]{:S(2)}, u32[]{:S(2)}) collective-permute-start(bf16[256,512]{0,1:T(8,128)(2,1)S(1)} %get-tuple-element.412), channel_id=1, source_target_pairs={{0,1},{1,2},{2,3},{3,4},{4,5},{5,6},{6,7},{7,8},{8,9},{9,10},{10,1... | collective-permute-start | bytes 786440 | tf_op jit(solution)/shard_map/while/body/eval_jaxpr/ppermute | solution.py:57
  253.4 12.8 %collective-permute-start.1 = (bf16[256,512]{0,1:T(8,128)(2,1)S(1)}, bf16[256,512]{0,1:T(8,128)(2,1)S(1)}, u32[]{:S(2)}, u32[]{:S(2)}) collective-permute-start(bf16[256,512]{0,1:T(8,128)(2,1)S(1)} %get-tuple-element.413), channel_id=1, source_target_pairs={{0,1},{1,2},{2,3},{3,4},{4,5},{5,6},{6,7},{7,8},{8,9},{9,10},{10,1... | collective-permute-start | bytes 786440 | tf_op jit(solution)/shard_map/while/body/eval_jaxpr/ppermute | solution.py:57
  263.4 2.8 copy-start.1
  269.5 11.9 %collective-permute-start = (bf16[256,512]{0,1:T(8,128)(2,1)S(1)}, bf16[256,512]{0,1:T(8,128)(2,1)S(1)}, u32[]{:S(2)}, u32[]{:S(2)}) collective-permute-start(bf16[256,512]{0,1:T(8,128)(2,1)S(1)} %get-tuple-element.412), channel_id=1, source_target_pairs={{0,1},{1,2},{2,3},{3,4},{4,5},{5,6},{6,7},{7,8},{8,9},{9,10},{10,1... | collective-permute-start | bytes 786440 | tf_op jit(solution)/shard_map/while/body/eval_jaxpr/ppermute | solution.py:57
  271.4 12.8 %collective-permute-start.1 = (bf16[256,512]{0,1:T(8,128)(2,1)S(1)}, bf16[256,512]{0,1:T(8,128)(2,1)S(1)}, u32[]{:S(2)}, u32[]{:S(2)}) collective-permute-start(bf16[256,512]{0,1:T(8,128)(2,1)S(1)} %get-tuple-element.413), channel_id=1, source_target_pairs={{0,1},{1,2},{2,3},{3,4},{4,5},{5,6},{6,7},{7,8},{8,9},{9,10},{10,1... | collective-permute-start | bytes 786440 | tf_op jit(solution)/shard_map/while/body/eval_jaxpr/ppermute | solution.py:57
  281.4 2.8 copy-start.1
  287.4 11.9 %collective-permute-start = (bf16[256,512]{0,1:T(8,128)(2,1)S(1)}, bf16[256,512]{0,1:T(8,128)(2,1)S(1)}, u32[]{:S(2)}, u32[]{:S(2)}) collective-permute-start(bf16[256,512]{0,1:T(8,128)(2,1)S(1)} %get-tuple-element.412), channel_id=1, source_target_pairs={{0,1},{1,2},{2,3},{3,4},{4,5},{5,6},{6,7},{7,8},{8,9},{9,10},{10,1... | collective-permute-start | bytes 786440 | tf_op jit(solution)/shard_map/while/body/eval_jaxpr/ppermute | solution.py:57
  289.3 12.8 %collective-permute-start.1 = (bf16[256,512]{0,1:T(8,128)(2,1)S(1)}, bf16[256,512]{0,1:T(8,128)(2,1)S(1)}, u32[]{:S(2)}, u32[]{:S(2)}) collective-permute-start(bf16[256,512]{0,1:T(8,128)(2,1)S(1)} %get-tuple-element.413), channel_id=1, source_target_pairs={{0,1},{1,2},{2,3},{3,4},{4,5},{5,6},{6,7},{7,8},{8,9},{9,10},{10,1... | collective-permute-start | bytes 786440 | tf_op jit(solution)/shard_map/while/body/eval_jaxpr/ppermute | solution.py:57
  299.3 2.8 copy-start.1
  305.4 11.9 %collective-permute-start = (bf16[256,512]{0,1:T(8,128)(2,1)S(1)}, bf16[256,512]{0,1:T(8,128)(2,1)S(1)}, u32[]{:S(2)}, u32[]{:S(2)}) collective-permute-start(bf16[256,512]{0,1:T(8,128)(2,1)S(1)} %get-tuple-element.412), channel_id=1, source_target_pairs={{0,1},{1,2},{2,3},{3,4},{4,5},{5,6},{6,7},{7,8},{8,9},{9,10},{10,1... | collective-permute-start | bytes 786440 | tf_op jit(solution)/shard_map/while/body/eval_jaxpr/ppermute | solution.py:57
  307.3 12.8 %collective-permute-start.1 = (bf16[256,512]{0,1:T(8,128)(2,1)S(1)}, bf16[256,512]{0,1:T(8,128)(2,1)S(1)}, u32[]{:S(2)}, u32[]{:S(2)}) collective-permute-start(bf16[256,512]{0,1:T(8,128)(2,1)S(1)} %get-tuple-element.413), channel_id=1, source_target_pairs={{0,1},{1,2},{2,3},{3,4},{4,5},{5,6},{6,7},{7,8},{8,9},{9,10},{10,1... | collective-permute-start | bytes 786440 | tf_op jit(solution)/shard_map/while/body/eval_jaxpr/ppermute | solution.py:57
  317.3 2.8 copy-start.1
  323.4 11.9 %collective-permute-start = (bf16[256,512]{0,1:T(8,128)(2,1)S(1)}, bf16[256,512]{0,1:T(8,128)(2,1)S(1)}, u32[]{:S(2)}, u32[]{:S(2)}) collective-permute-start(bf16[256,512]{0,1:T(8,128)(2,1)S(1)} %get-tuple-element.412), channel_id=1, source_target_pairs={{0,1},{1,2},{2,3},{3,4},{4,5},{5,6},{6,7},{7,8},{8,9},{9,10},{10,1... | collective-permute-start | bytes 786440 | tf_op jit(solution)/shard_map/while/body/eval_jaxpr/ppermute | solution.py:57
  325.3 12.8 %collective-permute-start.1 = (bf16[256,512]{0,1:T(8,128)(2,1)S(1)}, bf16[256,512]{0,1:T(8,128)(2,1)S(1)}, u32[]{:S(2)}, u32[]{:S(2)}) collective-permute-start(bf16[256,512]{0,1:T(8,128)(2,1)S(1)} %get-tuple-element.413), channel_id=1, source_target_pairs={{0,1},{1,2},{2,3},{3,4},{4,5},{5,6},{6,7},{7,8},{8,9},{9,10},{10,1... | collective-permute-start | bytes 786440 | tf_op jit(solution)/shard_map/while/body/eval_jaxpr/ppermute | solution.py:57
  335.3 2.8 copy-start.1
  341.3 11.9 %collective-permute-start = (bf16[256,512]{0,1:T(8,128)(2,1)S(1)}, bf16[256,512]{0,1:T(8,128)(2,1)S(1)}, u32[]{:S(2)}, u32[]{:S(2)}) collective-permute-start(bf16[256,512]{0,1:T(8,128)(2,1)S(1)} %get-tuple-element.412), channel_id=1, source_target_pairs={{0,1},{1,2},{2,3},{3,4},{4,5},{5,6},{6,7},{7,8},{8,9},{9,10},{10,1... | collective-permute-start | bytes 786440 | tf_op jit(solution)/shard_map/while/body/eval_jaxpr/ppermute | solution.py:57
  343.3 12.8 %collective-permute-start.1 = (bf16[256,512]{0,1:T(8,128)(2,1)S(1)}, bf16[256,512]{0,1:T(8,128)(2,1)S(1)}, u32[]{:S(2)}, u32[]{:S(2)}) collective-permute-start(bf16[256,512]{0,1:T(8,128)(2,1)S(1)} %get-tuple-element.413), channel_id=1, source_target_pairs={{0,1},{1,2},{2,3},{3,4},{4,5},{5,6},{6,7},{7,8},{8,9},{9,10},{10,1... | collective-permute-start | bytes 786440 | tf_op jit(solution)/shard_map/while/body/eval_jaxpr/ppermute | solution.py:57
  353.2 2.8 copy-start.1
  359.3 11.9 %collective-permute-start = (bf16[256,512]{0,1:T(8,128)(2,1)S(1)}, bf16[256,512]{0,1:T(8,128)(2,1)S(1)}, u32[]{:S(2)}, u32[]{:S(2)}) collective-permute-start(bf16[256,512]{0,1:T(8,128)(2,1)S(1)} %get-tuple-element.412), channel_id=1, source_target_pairs={{0,1},{1,2},{2,3},{3,4},{4,5},{5,6},{6,7},{7,8},{8,9},{9,10},{10,1... | collective-permute-start | bytes 786440 | tf_op jit(solution)/shard_map/while/body/eval_jaxpr/ppermute | solution.py:57
  361.2 12.8 %collective-permute-start.1 = (bf16[256,512]{0,1:T(8,128)(2,1)S(1)}, bf16[256,512]{0,1:T(8,128)(2,1)S(1)}, u32[]{:S(2)}, u32[]{:S(2)}) collective-permute-start(bf16[256,512]{0,1:T(8,128)(2,1)S(1)} %get-tuple-element.413), channel_id=1, source_target_pairs={{0,1},{1,2},{2,3},{3,4},{4,5},{5,6},{6,7},{7,8},{8,9},{9,10},{10,1... | collective-permute-start | bytes 786440 | tf_op jit(solution)/shard_map/while/body/eval_jaxpr/ppermute | solution.py:57
  371.2 2.8 copy-start.1
  377.3 11.9 %collective-permute-start = (bf16[256,512]{0,1:T(8,128)(2,1)S(1)}, bf16[256,512]{0,1:T(8,128)(2,1)S(1)}, u32[]{:S(2)}, u32[]{:S(2)}) collective-permute-start(bf16[256,512]{0,1:T(8,128)(2,1)S(1)} %get-tuple-element.412), channel_id=1, source_target_pairs={{0,1},{1,2},{2,3},{3,4},{4,5},{5,6},{6,7},{7,8},{8,9},{9,10},{10,1... | collective-permute-start | bytes 786440 | tf_op jit(solution)/shard_map/while/body/eval_jaxpr/ppermute | solution.py:57
  379.2 12.8 %collective-permute-start.1 = (bf16[256,512]{0,1:T(8,128)(2,1)S(1)}, bf16[256,512]{0,1:T(8,128)(2,1)S(1)}, u32[]{:S(2)}, u32[]{:S(2)}) collective-permute-start(bf16[256,512]{0,1:T(8,128)(2,1)S(1)} %get-tuple-element.413), channel_id=1, source_target_pairs={{0,1},{1,2},{2,3},{3,4},{4,5},{5,6},{6,7},{7,8},{8,9},{9,10},{10,1... | collective-permute-start | bytes 786440 | tf_op jit(solution)/shard_map/while/body/eval_jaxpr/ppermute | solution.py:57
  389.2 2.8 copy-start.1
  395.3 11.9 %collective-permute-start = (bf16[256,512]{0,1:T(8,128)(2,1)S(1)}, bf16[256,512]{0,1:T(8,128)(2,1)S(1)}, u32[]{:S(2)}, u32[]{:S(2)}) collective-permute-start(bf16[256,512]{0,1:T(8,128)(2,1)S(1)} %get-tuple-element.412), channel_id=1, source_target_pairs={{0,1},{1,2},{2,3},{3,4},{4,5},{5,6},{6,7},{7,8},{8,9},{9,10},{10,1... | collective-permute-start | bytes 786440 | tf_op jit(solution)/shard_map/while/body/eval_jaxpr/ppermute | solution.py:57
  397.2 12.8 %collective-permute-start.1 = (bf16[256,512]{0,1:T(8,128)(2,1)S(1)}, bf16[256,512]{0,1:T(8,128)(2,1)S(1)}, u32[]{:S(2)}, u32[]{:S(2)}) collective-permute-start(bf16[256,512]{0,1:T(8,128)(2,1)S(1)} %get-tuple-element.413), channel_id=1, source_target_pairs={{0,1},{1,2},{2,3},{3,4},{4,5},{5,6},{6,7},{7,8},{8,9},{9,10},{10,1... | collective-permute-start | bytes 786440 | tf_op jit(solution)/shard_map/while/body/eval_jaxpr/ppermute | solution.py:57
  413.2 11.9 %collective-permute-start = (bf16[256,512]{0,1:T(8,128)(2,1)S(1)}, bf16[256,512]{0,1:T(8,128)(2,1)S(1)}, u32[]{:S(2)}, u32[]{:S(2)}) collective-permute-start(bf16[256,512]{0,1:T(8,128)(2,1)S(1)} %get-tuple-element.412), channel_id=1, source_target_pairs={{0,1},{1,2},{2,3},{3,4},{4,5},{5,6},{6,7},{7,8},{8,9},{9,10},{10,1... | collective-permute-start | bytes 786440 | tf_op jit(solution)/shard_map/while/body/eval_jaxpr/ppermute | solution.py:57
  415.1 12.8 %collective-permute-start.1 = (bf16[256,512]{0,1:T(8,128)(2,1)S(1)}, bf16[256,512]{0,1:T(8,128)(2,1)S(1)}, u32[]{:S(2)}, u32[]{:S(2)}) collective-permute-start(bf16[256,512]{0,1:T(8,128)(2,1)S(1)} %get-tuple-element.413), channel_id=1, source_target_pairs={{0,1},{1,2},{2,3},{3,4},{4,5},{5,6},{6,7},{7,8},{8,9},{9,10},{10,1... | collective-permute-start | bytes 786440 | tf_op jit(solution)/shard_map/while/body/eval_jaxpr/ppermute | solution.py:57
  425.1 2.8 copy-start.1
  431.2 11.9 %collective-permute-start = (bf16[256,512]{0,1:T(8,128)(2,1)S(1)}, bf16[256,512]{0,1:T(8,128)(2,1)S(1)}, u32[]{:S(2)}, u32[]{:S(2)}) collective-permute-start(bf16[256,512]{0,1:T(8,128)(2,1)S(1)} %get-tuple-element.412), channel_id=1, source_target_pairs={{0,1},{1,2},{2,3},{3,4},{4,5},{5,6},{6,7},{7,8},{8,9},{9,10},{10,1... | collective-permute-start | bytes 786440 | tf_op jit(solution)/shard_map/while/body/eval_jaxpr/ppermute | solution.py:57
  433.1 12.8 %collective-permute-start.1 = (bf16[256,512]{0,1:T(8,128)(2,1)S(1)}, bf16[256,512]{0,1:T(8,128)(2,1)S(1)}, u32[]{:S(2)}, u32[]{:S(2)}) collective-permute-start(bf16[256,512]{0,1:T(8,128)(2,1)S(1)} %get-tuple-element.413), channel_id=1, source_target_pairs={{0,1},{1,2},{2,3},{3,4},{4,5},{5,6},{6,7},{7,8},{8,9},{9,10},{10,1... | collective-permute-start | bytes 786440 | tf_op jit(solution)/shard_map/while/body/eval_jaxpr/ppermute | solution.py:57
  443.1 2.8 copy-start.1
  449.2 11.9 %collective-permute-start = (bf16[256,512]{0,1:T(8,128)(2,1)S(1)}, bf16[256,512]{0,1:T(8,128)(2,1)S(1)}, u32[]{:S(2)}, u32[]{:S(2)}) collective-permute-start(bf16[256,512]{0,1:T(8,128)(2,1)S(1)} %get-tuple-element.412), channel_id=1, source_target_pairs={{0,1},{1,2},{2,3},{3,4},{4,5},{5,6},{6,7},{7,8},{8,9},{9,10},{10,1... | collective-permute-start | bytes 786440 | tf_op jit(solution)/shard_map/while/body/eval_jaxpr/ppermute | solution.py:57
  451.1 12.8 %collective-permute-start.1 = (bf16[256,512]{0,1:T(8,128)(2,1)S(1)}, bf16[256,512]{0,1:T(8,128)(2,1)S(1)}, u32[]{:S(2)}, u32[]{:S(2)}) collective-permute-start(bf16[256,512]{0,1:T(8,128)(2,1)S(1)} %get-tuple-element.413), channel_id=1, source_target_pairs={{0,1},{1,2},{2,3},{3,4},{4,5},{5,6},{6,7},{7,8},{8,9},{9,10},{10,1... | collective-permute-start | bytes 786440 | tf_op jit(solution)/shard_map/while/body/eval_jaxpr/ppermute | solution.py:57
  (19 other events, 28.8 us)
where the time goes:
time: 475 us; the launch traced here: 472 us
  waiting for transfers between devices  139 us (29%)
  between operations  117 us (25%)
  starting transfers between devices  62.4 us (13%)
  matrix products  51 us (11%)
  local copies, waits for them, and re-layouts  40 us (8%)
  blocking collectives  35 us (7%)
  other arithmetic  26.6 us (6%)
    ppermute x32, waiting for transfers between devices, from_behind(): return lax.ppermute(array, axis, pairs)  139 us
    ppermute x32, starting transfers between devices, from_behind(): return lax.ppermute(array, axis, pairs)  62.4 us
    dot_general x17, matrix products, attend(): jnp.einsum('kgtl,lkd->tkgd', weights, v_heads, preferred_element_type=jnp...  36 us
    unnamed x4, blocking collectives  35 us
    while x112, local copies, waits for them, and re-layouts  21 us
    reduce_sum x17, other arithmetic, attend(): total_new = total * factor + jnp.sum(expo, axis=-1)  17.6 us
    dot_general x17, matrix products, attend(): jnp.einsum('tkgd,lkd->kgtl', q_heads, k_heads, preferred_element_type=jnp...  15 us
  transfers between devices with their start and end apart: 32, of which 32 were waited for; matrix products, arithmetic and copies ran while one was open for 7% of the time, Pallas kernels for 0%

commit v1 on v0

v1 whole, which is shorter than its diff:
```python
import math

import jax
import jax.numpy as jnp
from jax import lax
from jax.experimental import pallas as pl
from jax.experimental.pallas import tpu as pltpu
from jax.sharding import Mesh
from jax.sharding import PartitionSpec as P

Q_HEADS = 16
KV_HEADS = 4
HEAD_DIM = 128
WINDOW = 4096
TOK = 256
MY_Q = 8
GROUP = 4
HALF_Q = MY_Q * HEAD_DIM
HALF_KV = 2 * HEAD_DIM
MSG_ROWS = TOK + 8
GRP_SEQ = ("grp", "seq_0", "seq_1", "seq_2")
N_DEV = 256
SCALE = math.log2(math.e) / math.sqrt(HEAD_DIM)
LN2 = math.log(2.0)
NEG = -1e30
ITEMS = 2 * MY_Q
IN_VMEM = pl.BlockSpec(memory_space=pltpu.VMEM)
LEAN = pltpu.CompilerParams(vmem_limit_bytes=16 << 20)
FAR = 1 << 20


def pack_kernel(core_ref, k_ref, v_ref, seg_ref, same_ref, cross_ref):
    core = core_ref[0]
    seg = jnp.broadcast_to(seg_ref[...].astype(jnp.float32), (8, TOK)).astype(jnp.bfloat16)
    seg = jnp.concatenate([seg, seg], axis=1)
    same_ref[TOK:, :] = seg
    cross_ref[TOK:, :] = seg
    for e in range(2):

        @pl.when(core == e)
        def _():
            for ref, h in ((same_ref, e), (cross_ref, 1 - e)):
                ref[:TOK, :HALF_KV] = k_ref[:, h * HALF_KV : (h + 1) * HALF_KV]
                ref[:TOK, HALF_KV:] = v_ref[:, h * HALF_KV : (h + 1) * HALF_KV]


def pack(core, keys, values, segments):
    msg = jax.ShapeDtypeStruct((MSG_ROWS, 2 * HALF_KV), jnp.bfloat16)
    return pl.pallas_call(
        pack_kernel,
        grid_spec=pltpu.PrefetchScalarGridSpec(
            num_scalar_prefetch=1,
            grid=(1,),
            in_specs=[
                pl.BlockSpec((TOK, 512), lambda i, s: (0, 0)),
                pl.BlockSpec((TOK, 512), lambda i, s: (0, 0)),
                pl.BlockSpec((1, TOK), lambda i, s: (0, 0)),
            ],
            out_specs=[
                pl.BlockSpec((MSG_ROWS, 512), lambda i, s: (0, 0)),
                pl.BlockSpec((MSG_ROWS, 512), lambda i, s: (0, 0)),
            ],
        ),
        out_shape=(msg, msg),
        name="pack",
    )(core, keys, values, segments)


def hold(array):
    return pltpu.with_memory_space_constraint(array, pltpu.VMEM)


def rows_to_cols(row):
    return jnp.transpose(jnp.broadcast_to(row, (128, TOK)))


def split_kernel(q_own, q_sib, out_ref):
    for i in range(ITEMS):
        ref = (q_own, q_sib)[i % 2]
        q = ref[:, i // 2 * 128 : (i // 2 + 1) * 128].astype(jnp.float32) * SCALE
        hi = q.astype(jnp.bfloat16)
        out_ref[i, :, :128] = hi
        out_ref[i, :, 128:] = (q - hi.astype(jnp.float32)).astype(jnp.bfloat16)


def split_queries(q_own, q_sib):
    return pl.pallas_call(
        split_kernel,
        in_specs=[IN_VMEM] * 2,
        out_specs=IN_VMEM,
        out_shape=pltpu.VMEM((ITEMS, TOK, 256), jnp.bfloat16),
        compiler_params=LEAN,
        name="split_queries",
    )(hold(q_own), hold(q_sib))


def attend_kernel(back, init, final, *refs):
    n = 2 * len(back)
    refs = list(refs)
    place_ref, q_ref = refs.pop(0), refs.pop(0)
    qmsg_refs = [refs.pop(0), refs.pop(0)]
    kv_refs = [refs.pop(0) for _ in range(n)]
    if not init:
        m_in, acc_in = refs.pop(0), refs.pop(0)
    if final:
        o_refs = [refs.pop(0), refs.pop(0)]
        lse_refs = [refs.pop(0), refs.pop(0)]
    else:
        m_out, acc_out = refs.pop(0), refs.pop(0)
    s_ref, top_ref = refs

    chip, core = place_ref[0], place_ref[1]
    side = (1 - 2 * core) * TOK

    def seg_row(ref):
        return ref[TOK : TOK + 1, :TOK].astype(jnp.float32)

    def columns(ref, first, g):
        return ref[:TOK, pl.ds(pl.multiple_of(first + g * 128, 128), 128)]

    def score(i, half, masked):
        g = i // (2 * GROUP)
        q2 = q_ref[i]
        keys = jnp.concatenate([columns(r, 0, g) for r in kv_refs], axis=0)
        keys = jnp.concatenate([keys, keys], axis=1)
        s = lax.dot_general(q2, keys, (((1,), (1,)), ((), ())), preferred_element_type=jnp.float32)
        tiles = [s[:, t * 128 : (t + 1) * 128] for t in range(2 * n)]
        if masked:
            qseg = rows_to_cols(seg_row(qmsg_refs[half]))
            qi = lax.broadcasted_iota(jnp.int32, (TOK, 128), 0)
            kj = lax.broadcasted_iota(jnp.int32, (TOK, 128), 1)
            for t in range(2 * n):
                b = t // 2
                k = back[b // 2]
                delta = (b % 2 - half) * side - 512 * k + (t % 2) * 128
                delta = jnp.where(chip >= k, delta, FAR)
                dist = kj - qi + delta
                kseg = seg_row(kv_refs[b])[:, t % 2 * 128 : (t % 2 + 1) * 128]
                ok = (dist <= 0) & (dist > -WINDOW) & (kseg == qseg)
                tiles[t] = jnp.where(ok, tiles[t], NEG)
        top = tiles[0]
        for t in range(2 * n):
            s_ref[half, :, t * 128 : (t + 1) * 128] = tiles[t]
            if t:
                top = jnp.maximum(top, tiles[t])
        top_ref[half] = jnp.broadcast_to(jnp.max(top, axis=1, keepdims=True), (TOK, 128))

    def combine(i, half):
        g = i // (2 * GROUP)
        vals = jnp.concatenate([columns(r, HALF_KV, g) for r in kv_refs], axis=0)
        vals = jnp.concatenate([vals, jnp.ones_like(vals)], axis=1)
        top = top_ref[half]
        if init:
            m = top
        else:
            m_old = m_in[i]
            m = jnp.maximum(m_old, top)
        p = jnp.concatenate(
            [
                jnp.exp2(s_ref[half, :, t * 128 : (t + 1) * 128] - m).astype(jnp.bfloat16)
                for t in range(2 * n)
            ],
            axis=1,
        )
        acc = jnp.dot(p, vals, preferred_element_type=jnp.float32)
        if not init:
            fac = jnp.exp2(m_old - m)
            acc = acc_in[i] * jnp.concatenate([fac, fac], axis=1) + acc
        if final:
            h = i // 2
            total = acc[:, 128:]
            at = pl.ds(pl.multiple_of(h * 128, 128), 128)
            o_refs[half][:, at] = (acc[:, :128] / total).astype(jnp.bfloat16)
            lse = LN2 * (m + jnp.log2(total))
            lse_refs[half][pl.ds(h, 1), :] = jnp.transpose(lse)[:1, :]
        else:
            m_out[i] = m
            acc_out[i] = acc

    def run(masked):
        score(0, 0, masked)

        def body(j, _):
            i = 2 * j
            score(i + 1, 1, masked)
            combine(i, 0)
            score(jnp.minimum(i + 2, ITEMS - 2), 0, masked)
            combine(i + 1, 1)
            return 0

        lax.fori_loop(0, ITEMS // 2, body, 0)

    if min(back) > 0 and max(back) < 8:
        low = seg_row(kv_refs[0])
        for ref in kv_refs[1:]:
            low = jnp.minimum(low, seg_row(ref))
        high = jnp.maximum(seg_row(qmsg_refs[0]), seg_row(qmsg_refs[1]))
        whole = (jnp.min(low) == jnp.max(high)) & (chip >= max(back))
        pl.when(whole)(lambda: run(False))
        pl.when(jnp.logical_not(whole))(lambda: run(True))
    else:
        run(True)


def attend(place, q2, qmsg, kv, back, state, final):
    init = state is None
    args = [q2, *qmsg, *kv]
    if not init:
        args += list(state)
    if final:
        out_shape = [pltpu.VMEM((TOK, HALF_Q), jnp.bfloat16)] * 2
        out_shape += [pltpu.VMEM((MY_Q, TOK), jnp.float32)] * 2
    else:
        out_shape = [
            pltpu.VMEM((ITEMS, TOK, 128), jnp.float32),
            pltpu.VMEM((ITEMS, TOK, 256), jnp.float32),
        ]
    size = ITEMS * TOK * TOK * len(kv)
    return pl.pallas_call(
        lambda *refs: attend_kernel(back, init, final, *refs),
        in_specs=[pl.BlockSpec(memory_space=pltpu.SMEM)] + [IN_VMEM] * len(args),
        out_specs=[IN_VMEM] * len(out_shape),
        out_shape=out_shape,
        input_output_aliases={} if init or final else {len(args) - 1: 0, len(args): 1},
        scratch_shapes=[
            pltpu.VMEM((2, TOK, TOK * len(kv)), jnp.float32),
            pltpu.VMEM((2, TOK, 128), jnp.float32),
        ],
        cost_estimate=pl.CostEstimate(
            flops=size * 1024, transcendentals=size, bytes_accessed=0
        ),
        compiler_params=LEAN,
        name="attend_" + "_".join(map(str, back)),
    )(place, *map(hold, args))


def chips_on(by, cross=False):
    flip = 1 if cross else 0
    return [(d, (d + 2 * by) % N_DEV ^ flip) for d in range(N_DEV)]


def on_device(queries, key_rows, value_rows, segments):
    device = lax.axis_index(GRP_SEQ)
    core = device % 2
    chip = device // 2
    place = jnp.stack([chip, core]).astype(jnp.int32)
    swap = [(d, d ^ 1) for d in range(N_DEV)]

    def move(array, pairs):
        return lax.ppermute(array, GRP_SEQ, pairs)

    same, cross = pack(core[None].astype(jnp.int32), key_rows, value_rows, segments[None, :])
    fwd = [move(same, chips_on(1)), move(cross, chips_on(1, True))]
    bwd = [move(same, chips_on(8)), move(cross, chips_on(8, True))]
    sib = move(cross, swap)
    q_low, q_high = queries[:, :HALF_Q], queries[:, HALF_Q:]
    q_mine = jnp.where(core == 0, q_low, q_high)
    q_sib = move(jnp.where(core == 0, q_high, q_low), swap)
    q, qmsg = split_queries(q_mine, q_sib), [same, sib]

    state = attend(place, q, qmsg, [same, sib], (0,), None, False)
    for step in range(1, 5):
        if step < 4:
            fwd_next = [move(x, chips_on(1)) for x in fwd]
            bwd_next = [move(x, chips_on(-1)) for x in bwd]
        far = 8 if step == 1 else 9 - step
        state = attend(place, q, qmsg, [*fwd, *bwd], (step, far), state, step == 4)
        if step < 4:
            fwd, bwd = fwd_next, bwd_next

    o_mine, o_sib, l_mine, l_sib = state
    o_other = move(o_sib, swap)
    l_other = move(l_sib, swap)
    first = core == 0
    attended = jnp.concatenate(
        [jnp.where(first, o_mine, o_other), jnp.where(first, o_other, o_mine)], axis=1
    )
    log_sums = jnp.concatenate(
        [jnp.where(first, l_mine, l_other), jnp.where(first, l_other, l_mine)], axis=0
    )
    return (attended, log_sums)


def solution(mesh):
    split = Mesh(
        mesh.devices.reshape(mesh.shape["grp"], 4, 8, 2), ("grp", "seq_0", "seq_1", "seq_2")
    )
    placed = (P(GRP_SEQ, None), P(GRP_SEQ, None), P(GRP_SEQ, None), P(GRP_SEQ))
    return jax.shard_map(
        on_device,
        mesh=split,
        in_specs=placed,
        out_specs=(P(GRP_SEQ, None), P(None, GRP_SEQ)),
        check_vma=False,
    )
```

time: 475 us -> 114 us (0.24)
  the two profiles are of different devices: /device:TPU:8 before, /device:TPU:1 now
where the time goes in v1:
time: 114 us
  Pallas kernels  52.9 us (46%)
  starting transfers between devices  33.6 us (29%)
  waiting for transfers between devices  23.2 us (20%)
  other arithmetic  3.09 us (3%)
    pallas_call x5, Pallas kernels, attend(): pl.pallas_call(lambda *refs: attend_kernel(back, init, final, *refs), in_...  50.6 us
    ppermute x20, starting transfers between devices, move(): return lax.ppermute(array, GRP_SEQ, pairs)  33.6 us
    ppermute x20, waiting for transfers between devices, move(): return lax.ppermute(array, GRP_SEQ, pairs)  23.2 us
  transfers between devices with their start and end apart: 20, of which 5 were waited for; matrix products, arithmetic and copies ran while one was open for 2% of the time, Pallas kernels for 35%

profile of v1, /device:TPU:1, one launch (start us, length us, event | category | flops | bytes accessed | tf_op | source)
XLA Modules:
  0.0 113.6 jit_solution(1497141371976952636)
XLA Ops:
  0.6 1.9 %pack.1 = (bf16[264,512]{1,0:T(8,128)(2,1)}, bf16[264,512]{1,0:T(8,128)(2,1)}) custom-call(s32[1]{0:T(128)} %bitcast.1.core_ref, bf16[256,512]{1,0:T(8,128)(2,1)} %k_ref.1, bf16[256,512]{1,0:T(8,128)(2,1)} %v_ref.1, s32[1,256]{1,0:T(1,128)} %bitcast.3), custom_call_target="tpu_custom_call" | custom-call | tf_op jit(solution)/shard_map/pack/pallas_call | solution.py:49
  2.5 2.0 %collective-permute-start.10 = (bf16[264,512]{1,0:T(8,128)(2,1)}, bf16[264,512]{1,0:T(8,128)(2,1)S(1)}, u32[]{:S(2)}, u32[]{:S(2)}) collective-permute-start(bf16[264,512]{1,0:T(8,128)(2,1)} %get-tuple-element.16.refs_2_.refs_4_), channel_id=1, source_target_pairs={{0,16},{1,17},{2,18},{3,19},{4,20},{5,21},{6,22},{7,23},{8,24},{9,... | collective-permute-start | bytes 811016 | tf_op jit(solution)/shard_map/ppermute | solution.py:250
  4.5 1.3 %broadcast_select_fusion.2 = (bf16[256,1024]{1,0:T(8,128)(2,1)S(1)}, bf16[256,1024]{1,0:T(8,128)(2,1)S(1)}) fusion(pred[]{:T(512)S(6)} %eq.4, bf16[256,2048]{1,0:T(8,128)(2,1)} %param.4), kind=kLoop, calls=%fused_computation.3 | loop fusion | flops 524288 | bytes 2097153 | tf_op jit(solution)/shard_map/jit(_where)/select_n | solution.py:258
  5.8 1.3 %collective-permute-start = (bf16[256,1024]{1,0:T(8,128)(2,1)S(1)}, bf16[256,1024]{1,0:T(8,128)(2,1)S(1)}, u32[]{:S(2)}, u32[]{:S(2)}) collective-permute-start(bf16[256,1024]{1,0:T(8,128)(2,1)S(1)} %get-tuple-element.32), channel_id=1, source_target_pairs={{0,1},{1,0},{2,3},{3,2},{4,5},{5,4},{6,7},{7,6},{8,9},{9,8},{10,11... | collective-permute-start | bytes 1572872 | tf_op jit(solution)/shard_map/ppermute | solution.py:250
  7.2 0.9 collective-permute-start.14
  8.1 1.6 %collective-permute-start.2 = (bf16[264,512]{1,0:T(8,128)(2,1)S(1)}, bf16[264,512]{1,0:T(8,128)(2,1)S(1)}, u32[]{:S(2)}, u32[]{:S(2)}) collective-permute-start(bf16[264,512]{1,0:T(8,128)(2,1)S(1)} %copy-done), channel_id=1, source_target_pairs={{0,2},{1,3},{2,4},{3,5},{4,6},{5,7},{6,8},{7,9},{8,10},{9,11},{10,... | collective-permute-start | bytes 811016 | tf_op jit(solution)/shard_map/ppermute | solution.py:250
  9.7 2.2 %collective-permute-start.6 = (bf16[264,512]{1,0:T(8,128)(2,1)S(1)}, bf16[264,512]{1,0:T(8,128)(2,1)S(1)}, u32[]{:S(2)}, u32[]{:S(2)}) collective-permute-start(bf16[264,512]{1,0:T(8,128)(2,1)S(1)} %copy-done.1), channel_id=1, source_target_pairs={{0,3},{1,2},{2,5},{3,4},{4,7},{5,6},{6,9},{7,8},{8,11},{9,10},{10,... | collective-permute-start | bytes 811016 | tf_op jit(solution)/shard_map/ppermute | solution.py:250
  11.9 1.0 collective-permute-done.10.refs_6_
  12.9 5.2 %collective-permute-start.1 = (bf16[264,512]{1,0:T(8,128)(2,1)S(1)}, bf16[264,512]{1,0:T(8,128)(2,1)S(1)}, u32[]{:S(2)}, u32[]{:S(2)}) collective-permute-start(bf16[264,512]{1,0:T(8,128)(2,1)S(1)} %copy-done.1), channel_id=1, source_target_pairs={{0,1},{1,0},{2,3},{3,2},{4,5},{5,4},{6,7},{7,6},{8,9},{9,8},{10,11... | collective-permute-start | bytes 811016 | tf_op jit(solution)/shard_map/ppermute | solution.py:250
  18.1 0.1 pad_add_fusion.refs_0_
  18.2 14.5 %collective-permute-done.14.refs_7_ = bf16[264,512]{1,0:T(8,128)(2,1)S(1)} collective-permute-done((bf16[264,512]{1,0:T(8,128)(2,1)S(1)}, bf16[264,512]{1,0:T(8,128)(2,1)S(1)}, u32[]{:S(2)}, u32[]{:S(2)}) %collective-permute-start.14) | collective-permute-done | bytes 270368 | tf_op jit(solution)/shard_map/ppermute | solution.py:250
  32.6 0.0 collective-permute-start.11
  32.6 0.0 collective-permute-done.2.refs_4_
  32.6 0.0 collective-permute-start.15
  32.6 0.0 collective-permute-done.6.refs_5_
  32.7 1.5 %collective-permute-start.3 = (bf16[264,512]{1,0:T(8,128)(2,1)S(1)}, bf16[264,512]{1,0:T(8,128)(2,1)S(1)}, u32[]{:S(2)}, u32[]{:S(2)}) collective-permute-start(bf16[264,512]{1,0:T(8,128)(2,1)S(1)} %collective-permute-done.2.refs_4_), channel_id=1, source_target_pairs={{0,2},{1,3},{2,4},{3,5},{4,6},{5,7},{6,8},{7,9},{8,10},{9,11},{10,... | collective-permute-start | bytes 811016 | tf_op jit(solution)/shard_map/ppermute | solution.py:250
  34.2 0.0 collective-permute-done.q_sib
  34.2 1.4 %collective-permute-start.7 = (bf16[264,512]{1,0:T(8,128)(2,1)S(1)}, bf16[264,512]{1,0:T(8,128)(2,1)S(1)}, u32[]{:S(2)}, u32[]{:S(2)}) collective-permute-start(bf16[264,512]{1,0:T(8,128)(2,1)S(1)} %collective-permute-done.6.refs_5_), channel_id=1, source_target_pairs={{0,2},{1,3},{2,4},{3,5},{4,6},{5,7},{6,8},{7,9},{8,10},{9,11},{10,... | collective-permute-start | bytes 811016 | tf_op jit(solution)/shard_map/ppermute | solution.py:250
  35.6 0.5 split_queries.1.refs_1_
  36.1 0.0 collective-permute-done.1.refs_3_.refs_5_
  36.1 6.8 %attend_0.1 = (f32[16,256,128]{2,1,0:T(8,128)S(1)}, f32[16,256,256]{2,1,0:T(8,128)S(1)}) custom-call(s32[2]{0:T(128)S(1)} %pad_add_fusion.refs_0_, bf16[16,256,256]{2,1,0:T(8,128)(2,1)S(1)} %split_queries.1.refs_1_, bf16[264,512]{1,0:T(8,128)(2,1)S(1)} %copy-done, bf16[264,512]{1,0:T(8,128)(2,1)S(1)} %collective-permute-done.1.refs_3_.refs_5_, ...), custom_call_target="tpu_custom_call" | custom-call | flops 2147483648 | tf_op jit(solution)/shard_map/attend_0/pallas_call | solution.py:219
  42.9 10.8 %attend_1_8.1 = (f32[16,256,128]{2,1,0:T(8,128)S(1)}, f32[16,256,256]{2,1,0:T(8,128)S(1)}) custom-call(s32[2]{0:T(128)S(1)} %pad_add_fusion.refs_0_, bf16[16,256,256]{2,1,0:T(8,128)(2,1)S(1)} %split_queries.1.refs_1_, bf16[264,512]{1,0:T(8,128)(2,1)S(1)} %copy-done, ...), custom_call_target="tpu_custom_call", output_to_operand_aliasing={{0}: (8, {}), {1}: (9, {})} | custom-call | flops 4294967296 | tf_op jit(solution)/shard_map/attend_1_8/pallas_call | solution.py:219
  53.7 0.0 collective-permute-done.11.refs_6_
  53.7 5.6 %collective-permute-start.12 = (bf16[264,512]{1,0:T(8,128)(2,1)S(1)}, bf16[264,512]{1,0:T(8,128)(2,1)S(1)}, u32[]{:S(2)}, u32[]{:S(2)}) collective-permute-start(bf16[264,512]{1,0:T(8,128)(2,1)S(1)} %collective-permute-done.11.refs_6_), channel_id=1, source_target_pairs={{0,254},{1,255},{2,0},{3,1},{4,2},{5,3},{6,4},{7,5},{8,6},{9,7},{1... | collective-permute-start | bytes 811016 | tf_op jit(solution)/shard_map/ppermute | solution.py:250
  59.3 0.0 collective-permute-done.15.refs_7_
  59.3 0.1 collective-permute-start.16
  59.4 0.0 collective-permute-done.3.refs_4_
  59.4 1.4 %collective-permute-start.4 = (bf16[264,512]{1,0:T(8,128)(2,1)S(1)}, bf16[264,512]{1,0:T(8,128)(2,1)S(1)}, u32[]{:S(2)}, u32[]{:S(2)}) collective-permute-start(bf16[264,512]{1,0:T(8,128)(2,1)S(1)} %collective-permute-done.3.refs_4_), channel_id=1, source_target_pairs={{0,2},{1,3},{2,4},{3,5},{4,6},{5,7},{6,8},{7,9},{8,10},{9,11},{10,... | collective-permute-start | bytes 811016 | tf_op jit(solution)/shard_map/ppermute | solution.py:250
  60.8 0.0 collective-permute-done.7.refs_5_
  60.8 0.1 collective-permute-start.8
  60.9 10.9 %attend_2_7.1 = (f32[16,256,128]{2,1,0:T(8,128)S(1)}, f32[16,256,256]{2,1,0:T(8,128)S(1)}) custom-call(s32[2]{0:T(128)S(1)} %pad_add_fusion.refs_0_, bf16[16,256,256]{2,1,0:T(8,128)(2,1)S(1)} %split_queries.1.refs_1_, bf16[264,512]{1,0:T(8,128)(2,1)S(1)} %copy-done, ...), custom_call_target="tpu_custom_call", output_to_operand_aliasing={{0}: (8, {}), {1}: (9, {})} | custom-call | flops 4294967296 | tf_op jit(solution)/shard_map/attend_2_7/pallas_call | solution.py:219
  71.8 6.9 %collective-permute-start.13 = (bf16[264,512]{1,0:T(8,128)(2,1)S(1)}, bf16[264,512]{1,0:T(8,128)(2,1)S(1)}, u32[]{:S(2)}, u32[]{:S(2)}) collective-permute-start(bf16[264,512]{1,0:T(8,128)(2,1)S(1)} %collective-permute-done.12.refs_6_), channel_id=1, source_target_pairs={{0,254},{1,255},{2,0},{3,1},{4,2},{5,3},{6,4},{7,5},{8,6},{9,7},{1... | collective-permute-start | bytes 811016 | tf_op jit(solution)/shard_map/ppermute | solution.py:250
  78.7 0.3 collective-permute-start.17
  78.9 0.0 collective-permute-done.4.refs_4_
  78.9 1.2 %collective-permute-start.5 = (bf16[264,512]{1,0:T(8,128)(2,1)S(1)}, bf16[264,512]{1,0:T(8,128)(2,1)S(1)}, u32[]{:S(2)}, u32[]{:S(2)}) collective-permute-start(bf16[264,512]{1,0:T(8,128)(2,1)S(1)} %collective-permute-done.4.refs_4_), channel_id=1, source_target_pairs={{0,2},{1,3},{2,4},{3,5},{4,6},{5,7},{6,8},{7,9},{8,10},{9,11},{10,... | collective-permute-start | bytes 811016 | tf_op jit(solution)/shard_map/ppermute | solution.py:250
  80.2 0.0 collective-permute-done.8.refs_5_
  80.2 0.1 collective-permute-start.9
  80.2 10.9 %attend_3_6.1 = (f32[16,256,128]{2,1,0:T(8,128)S(1)}, f32[16,256,256]{2,1,0:T(8,128)S(1)}) custom-call(s32[2]{0:T(128)S(1)} %pad_add_fusion.refs_0_, bf16[16,256,256]{2,1,0:T(8,128)(2,1)S(1)} %split_queries.1.refs_1_, bf16[264,512]{1,0:T(8,128)(2,1)S(1)} %copy-done, ...), custom_call_target="tpu_custom_call", output_to_operand_aliasing={{0}: (8, {}), {1}: (9, {})} | custom-call | flops 4294967296 | tf_op jit(solution)/shard_map/attend_3_6/pallas_call | solution.py:219
  91.2 0.0 collective-permute-done.17.refs_7_
  91.2 0.5 collective-permute-done.5.refs_4_
  91.6 5.8 %collective-permute-done.9.refs_5_ = bf16[264,512]{1,0:T(8,128)(2,1)S(1)} collective-permute-done((bf16[264,512]{1,0:T(8,128)(2,1)S(1)}, bf16[264,512]{1,0:T(8,128)(2,1)S(1)}, u32[]{:S(2)}, u32[]{:S(2)}) %collective-permute-start.9) | collective-permute-done | bytes 270368 | tf_op jit(solution)/shard_map/ppermute | solution.py:250
  97.4 11.1 %attend_4_5.1 = (bf16[256,1024]{1,0:T(8,128)(2,1)S(1)}, bf16[256,1024]{1,0:T(8,128)(2,1)S(1)}, f32[8,256]{1,0:T(8,128)S(1)}, f32[8,256]{1,0:T(8,128)S(1)}) custom-call(s32[2]{0:T(128)S(1)} %pad_add_fusion.refs_0_, bf16[16,256,256]{2,1,0:T(8,128)(2,1)S(1)} %split_queries.1.refs_1_, bf16[264,512]{1,0:T(8,128)(2,1)S(1)} %copy-done, ...), custom_call_target="tpu_custom_call" | custom-call | flops 4294967296 | tf_op jit(solution)/shard_map/attend_4_5/pallas_call | solution.py:219
  108.6 1.7 %collective-permute-start.18 = (bf16[256,1024]{1,0:T(8,128)(2,1)S(1)}, bf16[256,1024]{1,0:T(8,128)(2,1)S(1)}, u32[]{:S(2)}, u32[]{:S(2)}) collective-permute-start(bf16[256,1024]{1,0:T(8,128)(2,1)S(1)} %get-tuple-element.27), channel_id=1, source_target_pairs={{0,1},{1,0},{2,3},{3,2},{4,5},{5,4},{6,7},{7,6},{8,9},{9,8},{10,11... | collective-permute-start | bytes 1572872 | tf_op jit(solution)/shard_map/ppermute | solution.py:250
  110.3 0.1 collective-permute-start.19
  110.4 1.4 %collective-permute-done.19 = f32[8,256]{1,0:T(8,128)S(1)} collective-permute-done((f32[8,256]{1,0:T(8,128)S(1)}, f32[8,256]{1,0:T(8,128)S(1)}, u32[]{:S(2)}, u32[]{:S(2)}) %collective-permute-start.19) | collective-permute-done | bytes 8224 | tf_op jit(solution)/shard_map/ppermute | solution.py:250
  111.8 0.6 pad_maximum_fusion.1
  112.4 0.1 broadcast_select_fusion.1
  112.5 1.1 pad_maximum_fusion
  (9 shorter events, 0.0 us)
Async XLA Ops:
  2.5 4.6 %copy-start.1 = (bf16[264,512]{1,0:T(8,128)(2,1)S(1)}, bf16[264,512]{1,0:T(8,128)(2,1)}, u32[]{:S(2)}) copy-start(bf16[264,512]{1,0:T(8,128)(2,1)} %get-tuple-element.17) | copy-start | bytes 811012
  2.5 5.5 %copy-start = (bf16[264,512]{1,0:T(8,128)(2,1)S(1)}, bf16[264,512]{1,0:T(8,128)(2,1)}, u32[]{:S(2)}) copy-start(bf16[264,512]{1,0:T(8,128)(2,1)} %get-tuple-element.16.refs_2_.refs_4_) | copy-start | bytes 811012
  2.5 10.4 %collective-permute-start.10 = (bf16[264,512]{1,0:T(8,128)(2,1)}, bf16[264,512]{1,0:T(8,128)(2,1)S(1)}, u32[]{:S(2)}, u32[]{:S(2)}) collective-permute-start(bf16[264,512]{1,0:T(8,128)(2,1)} %get-tuple-element.16.refs_2_.refs_4_), channel_id=1, source_target_pairs={{0,16},{1,17},{2,18},{3,19},{4,20},{5,21},{6,22},{7,23},{8,24},{9,... | collective-permute-start | bytes 811016 | tf_op jit(solution)/shard_map/ppermute | solution.py:250
  5.8 28.4 %collective-permute-start = (bf16[256,1024]{1,0:T(8,128)(2,1)S(1)}, bf16[256,1024]{1,0:T(8,128)(2,1)S(1)}, u32[]{:S(2)}, u32[]{:S(2)}) collective-permute-start(bf16[256,1024]{1,0:T(8,128)(2,1)S(1)} %get-tuple-element.32), channel_id=1, source_target_pairs={{0,1},{1,0},{2,3},{3,2},{4,5},{5,4},{6,7},{7,6},{8,9},{9,8},{10,11... | collective-permute-start | bytes 1572872 | tf_op jit(solution)/shard_map/ppermute | solution.py:250
  7.2 25.5 %collective-permute-start.14 = (bf16[264,512]{1,0:T(8,128)(2,1)S(1)}, bf16[264,512]{1,0:T(8,128)(2,1)S(1)}, u32[]{:S(2)}, u32[]{:S(2)}) collective-permute-start(bf16[264,512]{1,0:T(8,128)(2,1)S(1)} %copy-done.1), channel_id=1, source_target_pairs={{0,17},{1,16},{2,19},{3,18},{4,21},{5,20},{6,23},{7,22},{8,25},{9,... | collective-permute-start | bytes 811016 | tf_op jit(solution)/shard_map/ppermute | solution.py:250
  8.1 24.6 %collective-permute-start.2 = (bf16[264,512]{1,0:T(8,128)(2,1)S(1)}, bf16[264,512]{1,0:T(8,128)(2,1)S(1)}, u32[]{:S(2)}, u32[]{:S(2)}) collective-permute-start(bf16[264,512]{1,0:T(8,128)(2,1)S(1)} %copy-done), channel_id=1, source_target_pairs={{0,2},{1,3},{2,4},{3,5},{4,6},{5,7},{6,8},{7,9},{8,10},{9,11},{10,... | collective-permute-start | bytes 811016 | tf_op jit(solution)/shard_map/ppermute | solution.py:250
  9.7 22.9 %collective-permute-start.6 = (bf16[264,512]{1,0:T(8,128)(2,1)S(1)}, bf16[264,512]{1,0:T(8,128)(2,1)S(1)}, u32[]{:S(2)}, u32[]{:S(2)}) collective-permute-start(bf16[264,512]{1,0:T(8,128)(2,1)S(1)} %copy-done.1), channel_id=1, source_target_pairs={{0,3},{1,2},{2,5},{3,4},{4,7},{5,6},{6,9},{7,8},{8,11},{9,10},{10,... | collective-permute-start | bytes 811016 | tf_op jit(solution)/shard_map/ppermute | solution.py:250
  12.9 23.2 %collective-permute-start.1 = (bf16[264,512]{1,0:T(8,128)(2,1)S(1)}, bf16[264,512]{1,0:T(8,128)(2,1)S(1)}, u32[]{:S(2)}, u32[]{:S(2)}) collective-permute-start(bf16[264,512]{1,0:T(8,128)(2,1)S(1)} %copy-done.1), channel_id=1, source_target_pairs={{0,1},{1,0},{2,3},{3,2},{4,5},{5,4},{6,7},{7,6},{8,9},{9,8},{10,11... | collective-permute-start | bytes 811016 | tf_op jit(solution)/shard_map/ppermute | solution.py:250
  32.6 21.1 %collective-permute-start.11 = (bf16[264,512]{1,0:T(8,128)(2,1)S(1)}, bf16[264,512]{1,0:T(8,128)(2,1)S(1)}, u32[]{:S(2)}, u32[]{:S(2)}) collective-permute-start(bf16[264,512]{1,0:T(8,128)(2,1)S(1)} %collective-permute-done.10.refs_6_), channel_id=1, source_target_pairs={{0,254},{1,255},{2,0},{3,1},{4,2},{5,3},{6,4},{7,5},{8,6},{9,7},{1... | collective-permute-start | bytes 811016 | tf_op jit(solution)/shard_map/ppermute | solution.py:250
  32.6 26.7 %collective-permute-start.15 = (bf16[264,512]{1,0:T(8,128)(2,1)S(1)}, bf16[264,512]{1,0:T(8,128)(2,1)S(1)}, u32[]{:S(2)}, u32[]{:S(2)}) collective-permute-start(bf16[264,512]{1,0:T(8,128)(2,1)S(1)} %collective-permute-done.14.refs_7_), channel_id=1, source_target_pairs={{0,254},{1,255},{2,0},{3,1},{4,2},{5,3},{6,4},{7,5},{8,6},{9,7},{1... | collective-permute-start | bytes 811016 | tf_op jit(solution)/shard_map/ppermute | solution.py:250
  32.7 26.8 %collective-permute-start.3 = (bf16[264,512]{1,0:T(8,128)(2,1)S(1)}, bf16[264,512]{1,0:T(8,128)(2,1)S(1)}, u32[]{:S(2)}, u32[]{:S(2)}) collective-permute-start(bf16[264,512]{1,0:T(8,128)(2,1)S(1)} %collective-permute-done.2.refs_4_), channel_id=1, source_target_pairs={{0,2},{1,3},{2,4},{3,5},{4,6},{5,7},{6,8},{7,9},{8,10},{9,11},{10,... | collective-permute-start | bytes 811016 | tf_op jit(solution)/shard_map/ppermute | solution.py:250
  34.2 26.6 %collective-permute-start.7 = (bf16[264,512]{1,0:T(8,128)(2,1)S(1)}, bf16[264,512]{1,0:T(8,128)(2,1)S(1)}, u32[]{:S(2)}, u32[]{:S(2)}) collective-permute-start(bf16[264,512]{1,0:T(8,128)(2,1)S(1)} %collective-permute-done.6.refs_5_), channel_id=1, source_target_pairs={{0,2},{1,3},{2,4},{3,5},{4,6},{5,7},{6,8},{7,9},{8,10},{9,11},{10,... | collective-permute-start | bytes 811016 | tf_op jit(solution)/shard_map/ppermute | solution.py:250
  53.7 18.0 %collective-permute-start.12 = (bf16[264,512]{1,0:T(8,128)(2,1)S(1)}, bf16[264,512]{1,0:T(8,128)(2,1)S(1)}, u32[]{:S(2)}, u32[]{:S(2)}) collective-permute-start(bf16[264,512]{1,0:T(8,128)(2,1)S(1)} %collective-permute-done.11.refs_6_), channel_id=1, source_target_pairs={{0,254},{1,255},{2,0},{3,1},{4,2},{5,3},{6,4},{7,5},{8,6},{9,7},{1... | collective-permute-start | bytes 811016 | tf_op jit(solution)/shard_map/ppermute | solution.py:250
  59.3 19.4 %collective-permute-start.16 = (bf16[264,512]{1,0:T(8,128)(2,1)S(1)}, bf16[264,512]{1,0:T(8,128)(2,1)S(1)}, u32[]{:S(2)}, u32[]{:S(2)}) collective-permute-start(bf16[264,512]{1,0:T(8,128)(2,1)S(1)} %collective-permute-done.15.refs_7_), channel_id=1, source_target_pairs={{0,254},{1,255},{2,0},{3,1},{4,2},{5,3},{6,4},{7,5},{8,6},{9,7},{1... | collective-permute-start | bytes 811016 | tf_op jit(solution)/shard_map/ppermute | solution.py:250
  59.4 19.5 %collective-permute-start.4 = (bf16[264,512]{1,0:T(8,128)(2,1)S(1)}, bf16[264,512]{1,0:T(8,128)(2,1)S(1)}, u32[]{:S(2)}, u32[]{:S(2)}) collective-permute-start(bf16[264,512]{1,0:T(8,128)(2,1)S(1)} %collective-permute-done.3.refs_4_), channel_id=1, source_target_pairs={{0,2},{1,3},{2,4},{3,5},{4,6},{5,7},{6,8},{7,9},{8,10},{9,11},{10,... | collective-permute-start | bytes 811016 | tf_op jit(solution)/shard_map/ppermute | solution.py:250
  60.8 19.4 %collective-permute-start.8 = (bf16[264,512]{1,0:T(8,128)(2,1)S(1)}, bf16[264,512]{1,0:T(8,128)(2,1)S(1)}, u32[]{:S(2)}, u32[]{:S(2)}) collective-permute-start(bf16[264,512]{1,0:T(8,128)(2,1)S(1)} %collective-permute-done.7.refs_5_), channel_id=1, source_target_pairs={{0,2},{1,3},{2,4},{3,5},{4,6},{5,7},{6,8},{7,9},{8,10},{9,11},{10,... | collective-permute-start | bytes 811016 | tf_op jit(solution)/shard_map/ppermute | solution.py:250
  71.8 19.4 %collective-permute-start.13 = (bf16[264,512]{1,0:T(8,128)(2,1)S(1)}, bf16[264,512]{1,0:T(8,128)(2,1)S(1)}, u32[]{:S(2)}, u32[]{:S(2)}) collective-permute-start(bf16[264,512]{1,0:T(8,128)(2,1)S(1)} %collective-permute-done.12.refs_6_), channel_id=1, source_target_pairs={{0,254},{1,255},{2,0},{3,1},{4,2},{5,3},{6,4},{7,5},{8,6},{9,7},{1... | collective-permute-start | bytes 811016 | tf_op jit(solution)/shard_map/ppermute | solution.py:250
  78.7 12.5 %collective-permute-start.17 = (bf16[264,512]{1,0:T(8,128)(2,1)S(1)}, bf16[264,512]{1,0:T(8,128)(2,1)S(1)}, u32[]{:S(2)}, u32[]{:S(2)}) collective-permute-start(bf16[264,512]{1,0:T(8,128)(2,1)S(1)} %collective-permute-done.16.refs_7_), channel_id=1, source_target_pairs={{0,254},{1,255},{2,0},{3,1},{4,2},{5,3},{6,4},{7,5},{8,6},{9,7},{1... | collective-permute-start | bytes 811016 | tf_op jit(solution)/shard_map/ppermute | solution.py:250
  78.9 12.7 %collective-permute-start.5 = (bf16[264,512]{1,0:T(8,128)(2,1)S(1)}, bf16[264,512]{1,0:T(8,128)(2,1)S(1)}, u32[]{:S(2)}, u32[]{:S(2)}) collective-permute-start(bf16[264,512]{1,0:T(8,128)(2,1)S(1)} %collective-permute-done.4.refs_4_), channel_id=1, source_target_pairs={{0,2},{1,3},{2,4},{3,5},{4,6},{5,7},{6,8},{7,9},{8,10},{9,11},{10,... | collective-permute-start | bytes 811016 | tf_op jit(solution)/shard_map/ppermute | solution.py:250
  80.2 17.3 %collective-permute-start.9 = (bf16[264,512]{1,0:T(8,128)(2,1)S(1)}, bf16[264,512]{1,0:T(8,128)(2,1)S(1)}, u32[]{:S(2)}, u32[]{:S(2)}) collective-permute-start(bf16[264,512]{1,0:T(8,128)(2,1)S(1)} %collective-permute-done.8.refs_5_), channel_id=1, source_target_pairs={{0,2},{1,3},{2,4},{3,5},{4,6},{5,7},{6,8},{7,9},{8,10},{9,11},{10,... | collective-permute-start | bytes 811016 | tf_op jit(solution)/shard_map/ppermute | solution.py:250
  108.6 3.9 %collective-permute-start.18 = (bf16[256,1024]{1,0:T(8,128)(2,1)S(1)}, bf16[256,1024]{1,0:T(8,128)(2,1)S(1)}, u32[]{:S(2)}, u32[]{:S(2)}) collective-permute-start(bf16[256,1024]{1,0:T(8,128)(2,1)S(1)} %get-tuple-element.27), channel_id=1, source_target_pairs={{0,1},{1,0},{2,3},{3,2},{4,5},{5,4},{6,7},{7,6},{8,9},{9,8},{10,11... | collective-permute-start | bytes 1572872 | tf_op jit(solution)/shard_map/ppermute | solution.py:250
  110.3 1.5 %collective-permute-start.19 = (f32[8,256]{1,0:T(8,128)S(1)}, f32[8,256]{1,0:T(8,128)S(1)}, u32[]{:S(2)}, u32[]{:S(2)}) collective-permute-start(f32[8,256]{1,0:T(8,128)S(1)} %get-tuple-element.29), channel_id=1, source_target_pairs={{0,1},{1,0},{2,3},{3,2},{4,5},{5,4},{6,7},{7,6},{8,9},{9,8},{10,11... | collective-permute-start | bytes 24584 | tf_op jit(solution)/shard_map/ppermute | solution.py:250
